TPU v7x, 32 devices: a whole 2x2x4 slice. The times are simulated.
32 devices in a mesh: dp: 2 (over x), tp: 4 (over z), pp: 4 (over y, core).
Axes of the slice: x: 2, y: 2, z: 4, core: 2. Of those that a mesh axis runs over, the one named last changes fastest.
Arguments:
- hidden_in: bfloat16 [16, 512, 2048], P('dp', 'tp'), parts along dimension 0
- seg_ids: int32 [16, 512], P('dp'), parts along dimension 0
- positions: int32 [16, 512], P('dp'), parts along dimension 0
- attn_norm: bfloat16 [4, 2048], P('pp')
- w_query: bfloat16 [4, 2048, 2048], P('pp', None, 'tp')
- w_key: bfloat16 [4, 2048, 2048], P('pp', None, 'tp')
- w_value: bfloat16 [4, 2048, 2048], P('pp', None, 'tp')
- w_out: bfloat16 [4, 2048, 2048], P('pp', 'tp')
- mlp_norm: bfloat16 [4, 2048], P('pp')
- w_gate: bfloat16 [4, 2048, 8192], P('pp', None, 'tp')
- w_up: bfloat16 [4, 2048, 8192], P('pp', None, 'tp')
- w_down: bfloat16 [4, 8192, 2048], P('pp', 'tp')
Outputs:
- output: bfloat16 [16, 512, 2048], P('dp', 'tp'), parts along dimension 0
There are 2 independent parts. A program takes and returns all parts, laid end to end along the dimension named above; an argument that names none is the same for every part.
All inputs are finite; a program needn't handle non-finite values.
Results may differ from a plain program's by a relative error of at most 0.02.
Values are sent between devices in bfloat16 or wider.
A program may use at most 1 GiB of HBM per device.

v0:
```python
import math
import jax
import jax.numpy as jnp
from jax import lax
from jax.sharding import PartitionSpec as P

HEAD_DIM = 128
NORM_EPS = 1e-5
ROPE_THETA = 500000.0
ROPE_FACTOR = 8.0
LOW_FREQ = 1.0
HIGH_FREQ = 4.0
ORIG_CTX = 8192.0
QUERY_BLOCK = 512


def rope_freqs():
    table = []
    for index in range(HEAD_DIM // 2):
        base_freq = 1.0 / (ROPE_THETA ** (2 * index / HEAD_DIM))
        wavelen = 2.0 * math.pi / base_freq
        smooth = (ORIG_CTX / wavelen - LOW_FREQ) / (HIGH_FREQ - LOW_FREQ)
        if wavelen < ORIG_CTX / HIGH_FREQ:
            table.append(base_freq)
        elif wavelen > ORIG_CTX / LOW_FREQ:
            table.append(base_freq / ROPE_FACTOR)
        else:
            table.append((1.0 - smooth) * base_freq / ROPE_FACTOR + smooth * base_freq)
    return jnp.array(table, dtype=jnp.float32)


def rms_norm(hidden, gain):
    hidden_f = hidden.astype(jnp.float32)
    inv_rms = lax.rsqrt(jnp.mean(hidden_f * hidden_f, axis=-1, keepdims=True) + NORM_EPS)
    return (hidden_f * inv_rms * gain.astype(jnp.float32)).astype(jnp.bfloat16)


def apply_rope(proj, cos_tab, sin_tab):
    half_dim = proj.shape[-1] // 2
    lead_part = proj[..., :half_dim]
    tail_part = proj[..., half_dim:]
    cos_wide = cos_tab[..., None, :]
    sin_wide = sin_tab[..., None, :]
    return jnp.concatenate([lead_part * cos_wide - tail_part * sin_wide, tail_part * cos_wide + lead_part * sin_wide], axis=-1)


def attend(q_rot, k_rot, v_proj, seg_row):
    seq_len = q_rot.shape[0]
    n_heads = q_rot.shape[1]
    n_kv = k_rot.shape[1]
    block_rows = min(seq_len, QUERY_BLOCK)
    n_blocks = seq_len // block_rows
    q_blocks = q_rot.reshape(n_blocks, block_rows, n_kv, n_heads // n_kv, HEAD_DIM)
    seg_blocks = seg_row.reshape(n_blocks, block_rows)
    col_ids = jnp.arange(seq_len)
    row_blocks = col_ids.reshape(n_blocks, block_rows)
    score_scale = HEAD_DIM ** -0.5

    def one_block(blk_args):
        q_blk, seg_blk, row_blk = blk_args
        scores = jnp.einsum('qngd,knd->ngqk', q_blk, k_rot, preferred_element_type=jnp.float32) * score_scale
        allowed = (seg_blk[:, None] == seg_row[None, :]) & (row_blk[:, None] >= col_ids[None, :])
        scores = jnp.where(allowed, scores, -1e30)
        exp_scores = jnp.exp(scores - jnp.max(scores, axis=-1, keepdims=True))
        attn_probs = (exp_scores / jnp.sum(exp_scores, axis=-1, keepdims=True)).astype(jnp.bfloat16)
        context = jnp.einsum('ngqk,knd->qngd', attn_probs, v_proj, preferred_element_type=jnp.float32)
        return context.astype(jnp.bfloat16).reshape(block_rows, n_heads * HEAD_DIM)

    return lax.map(one_block, (q_blocks, seg_blocks, row_blocks)).reshape(seq_len, n_heads * HEAD_DIM)


def stage_layer(hidden, weights, cos_tab, sin_tab, seg_row):
    gain_attn, w_query, w_key, w_value, w_out, gain_mlp, w_gate, w_up, w_down = weights
    seq_len = cos_tab.shape[0]
    full_in = lax.all_gather(rms_norm(hidden, gain_attn), 'tp', axis=0, tiled=True)
    q_rot = apply_rope(jnp.dot(full_in, w_query, preferred_element_type=jnp.float32).reshape(seq_len, -1, HEAD_DIM), cos_tab, sin_tab).astype(jnp.bfloat16)
    k_rot = apply_rope(jnp.dot(full_in, w_key, preferred_element_type=jnp.float32).reshape(seq_len, -1, HEAD_DIM), cos_tab, sin_tab).astype(jnp.bfloat16)
    v_proj = jnp.dot(full_in, w_value, preferred_element_type=jnp.float32).astype(jnp.bfloat16).reshape(seq_len, -1, HEAD_DIM)
    attn_part = jnp.dot(attend(q_rot, k_rot, v_proj, seg_row), w_out, preferred_element_type=jnp.float32).astype(jnp.bfloat16)
    attn_out = lax.psum_scatter(attn_part, 'tp', scatter_dimension=0, tiled=True)
    mid_state = (hidden.astype(jnp.float32) + attn_out.astype(jnp.float32)).astype(jnp.bfloat16)
    full_mlp = lax.all_gather(rms_norm(mid_state, gain_mlp), 'tp', axis=0, tiled=True)
    gate_proj = jnp.dot(full_mlp, w_gate, preferred_element_type=jnp.float32)
    up_proj = jnp.dot(full_mlp, w_up, preferred_element_type=jnp.float32)
    hidden_act = (jax.nn.silu(gate_proj) * up_proj).astype(jnp.bfloat16)
    down_part = jnp.dot(hidden_act, w_down, preferred_element_type=jnp.float32).astype(jnp.bfloat16)
    down_out = lax.psum_scatter(down_part, 'tp', scatter_dimension=0, tiled=True)
    return (mid_state.astype(jnp.float32) + down_out.astype(jnp.float32)).astype(jnp.bfloat16)


def solution(mesh):
    n_stages = mesh.shape['pp']
    inv_freq = rope_freqs()
    fwd_perm = [(src, src + 1) for src in range(n_stages - 1)]

    def stage_program(hidden_in, seg_ids, positions, attn_norm, w_query, w_key, w_value, w_out, mlp_norm, w_gate, w_up, w_down):
        weights = (attn_norm[0], w_query[0], w_key[0], w_value[0], w_out[0], mlp_norm[0], w_gate[0], w_up[0], w_down[0])
        n_micro = hidden_in.shape[0]
        stage_idx = lax.axis_index('pp')
        is_first = stage_idx == 0
        is_last = stage_idx == n_stages - 1

        def stage_tick(recv_buf, step_idx):
            mb_index = jnp.clip(step_idx - stage_idx, 0, n_micro - 1)
            own_in = lax.dynamic_index_in_dim(hidden_in, mb_index, axis=0, keepdims=False)
            layer_in = jnp.where(is_first, own_in, recv_buf)
            seg_row = lax.dynamic_index_in_dim(seg_ids, mb_index, axis=0, keepdims=False)
            pos_row = lax.dynamic_index_in_dim(positions, mb_index, axis=0, keepdims=False)
            angles = pos_row.astype(jnp.float32)[:, None] * inv_freq[None, :]
            layer_out = stage_layer(layer_in, weights, jnp.cos(angles), jnp.sin(angles), seg_row)
            return lax.ppermute(layer_out, 'pp', perm=fwd_perm), layer_out

        first_buf = jnp.zeros_like(hidden_in[0])
        _, step_outs = lax.scan(stage_tick, first_buf, jnp.arange(n_micro + n_stages - 1))
        results = step_outs[n_stages - 1:]
        return lax.psum(jnp.where(is_last, results, jnp.zeros_like(results)), 'pp')

    act_spec = P('dp', 'tp', None)
    row_spec = P('dp', None)
    gain_spec = P('pp', None)
    col_spec = P('pp', None, 'tp')
    rows_spec = P('pp', 'tp', None)
    return jax.shard_map(stage_program, mesh=mesh,
                         in_specs=(act_spec, row_spec, row_spec, gain_spec, col_spec, col_spec, col_spec, rows_spec, gain_spec, col_spec, col_spec, rows_spec),
                         out_specs=act_spec, check_vma=False)
```

profile of v0, /device:TPU:25, one launch (start us, length us, event | category | flops | bytes accessed | tf_op | source)
XLA Modules:
  0.0 2809.6 jit_solution(5208937511859393797)
XLA Ops:
  8.9 2697.8 %while.12 = (s32[]{:T(128)}, bf16[128,2048]{1,0:T(8,128)(2,1)S(1)}, bf16[11,128,2048]{2,1,0:T(8,128)(2,1)}, pred[]{:T(512)}, s32[11]{0:T(128)S(1)}, /*index=5*/s...) while((s32[]{:T(128)}, bf16[128,2048]{1,0:T(8,128)(2,1)S(1)}, ...), condition=%wide.region_7.8_spmd.clone, body=%wide.region_0.7_spmd.sunk.clone.sunk | while | flops 17751375872 | bytes 164726080 | solution.py:114
  125.7 44.8 %all-gather.5.cloned.1.call-done = bf16[512,2048]{1,0:T(8,128)(2,1)} async-done(((bf16[128,2048]{1,0:T(8,128)(2,1)}), bf16[512,2048]{1,0:T(8,128)(2,1)}) %all-gather.5.cloned.1.call-update) | async-done | bytes 2097168 | tf_op jit(solution)/shard_map/while/body/eval_jaxpr/all_gather | solution.py:82
  198.7 42.6 %reduce-scatter.5.cloned.1.call-done = bf16[128,2048]{1,0:T(8,128)(2,1)} async-done(((bf16[512,2048]{1,0:T(8,128)(2,1)}), bf16[128,2048]{1,0:T(8,128)(2,1)}) %reduce-scatter.5.cloned.1.call-update) | async-done | bytes 524304 | tf_op jit(solution)/shard_map/while/body/eval_jaxpr/reduce_scatter | solution.py:87
  370.9 44.8 %all-gather.5.cloned.1.call-done = bf16[512,2048]{1,0:T(8,128)(2,1)} async-done(((bf16[128,2048]{1,0:T(8,128)(2,1)}), bf16[512,2048]{1,0:T(8,128)(2,1)}) %all-gather.5.cloned.1.call-update) | async-done | bytes 2097168 | tf_op jit(solution)/shard_map/while/body/eval_jaxpr/all_gather | solution.py:82
  443.9 42.6 %reduce-scatter.5.cloned.1.call-done = bf16[128,2048]{1,0:T(8,128)(2,1)} async-done(((bf16[512,2048]{1,0:T(8,128)(2,1)}), bf16[128,2048]{1,0:T(8,128)(2,1)}) %reduce-scatter.5.cloned.1.call-update) | async-done | bytes 524304 | tf_op jit(solution)/shard_map/while/body/eval_jaxpr/reduce_scatter | solution.py:87
  616.2 44.8 %all-gather.5.cloned.1.call-done = bf16[512,2048]{1,0:T(8,128)(2,1)} async-done(((bf16[128,2048]{1,0:T(8,128)(2,1)}), bf16[512,2048]{1,0:T(8,128)(2,1)}) %all-gather.5.cloned.1.call-update) | async-done | bytes 2097168 | tf_op jit(solution)/shard_map/while/body/eval_jaxpr/all_gather | solution.py:82
  689.2 42.6 %reduce-scatter.5.cloned.1.call-done = bf16[128,2048]{1,0:T(8,128)(2,1)} async-done(((bf16[512,2048]{1,0:T(8,128)(2,1)}), bf16[128,2048]{1,0:T(8,128)(2,1)}) %reduce-scatter.5.cloned.1.call-update) | async-done | bytes 524304 | tf_op jit(solution)/shard_map/while/body/eval_jaxpr/reduce_scatter | solution.py:87
  861.6 44.8 %all-gather.5.cloned.1.call-done = bf16[512,2048]{1,0:T(8,128)(2,1)} async-done(((bf16[128,2048]{1,0:T(8,128)(2,1)}), bf16[512,2048]{1,0:T(8,128)(2,1)}) %all-gather.5.cloned.1.call-update) | async-done | bytes 2097168 | tf_op jit(solution)/shard_map/while/body/eval_jaxpr/all_gather | solution.py:82
  934.5 42.6 %reduce-scatter.5.cloned.1.call-done = bf16[128,2048]{1,0:T(8,128)(2,1)} async-done(((bf16[512,2048]{1,0:T(8,128)(2,1)}), bf16[128,2048]{1,0:T(8,128)(2,1)}) %reduce-scatter.5.cloned.1.call-update) | async-done | bytes 524304 | tf_op jit(solution)/shard_map/while/body/eval_jaxpr/reduce_scatter | solution.py:87
  1106.8 44.8 %all-gather.5.cloned.1.call-done = bf16[512,2048]{1,0:T(8,128)(2,1)} async-done(((bf16[128,2048]{1,0:T(8,128)(2,1)}), bf16[512,2048]{1,0:T(8,128)(2,1)}) %all-gather.5.cloned.1.call-update) | async-done | bytes 2097168 | tf_op jit(solution)/shard_map/while/body/eval_jaxpr/all_gather | solution.py:82
  1179.8 42.6 %reduce-scatter.5.cloned.1.call-done = bf16[128,2048]{1,0:T(8,128)(2,1)} async-done(((bf16[512,2048]{1,0:T(8,128)(2,1)}), bf16[128,2048]{1,0:T(8,128)(2,1)}) %reduce-scatter.5.cloned.1.call-update) | async-done | bytes 524304 | tf_op jit(solution)/shard_map/while/body/eval_jaxpr/reduce_scatter | solution.py:87
  1352.1 44.8 %all-gather.5.cloned.1.call-done = bf16[512,2048]{1,0:T(8,128)(2,1)} async-done(((bf16[128,2048]{1,0:T(8,128)(2,1)}), bf16[512,2048]{1,0:T(8,128)(2,1)}) %all-gather.5.cloned.1.call-update) | async-done | bytes 2097168 | tf_op jit(solution)/shard_map/while/body/eval_jaxpr/all_gather | solution.py:82
  1425.1 42.6 %reduce-scatter.5.cloned.1.call-done = bf16[128,2048]{1,0:T(8,128)(2,1)} async-done(((bf16[512,2048]{1,0:T(8,128)(2,1)}), bf16[128,2048]{1,0:T(8,128)(2,1)}) %reduce-scatter.5.cloned.1.call-update) | async-done | bytes 524304 | tf_op jit(solution)/shard_map/while/body/eval_jaxpr/reduce_scatter | solution.py:87
  1597.5 44.8 %all-gather.5.cloned.1.call-done = bf16[512,2048]{1,0:T(8,128)(2,1)} async-done(((bf16[128,2048]{1,0:T(8,128)(2,1)}), bf16[512,2048]{1,0:T(8,128)(2,1)}) %all-gather.5.cloned.1.call-update) | async-done | bytes 2097168 | tf_op jit(solution)/shard_map/while/body/eval_jaxpr/all_gather | solution.py:82
  1670.5 42.6 %reduce-scatter.5.cloned.1.call-done = bf16[128,2048]{1,0:T(8,128)(2,1)} async-done(((bf16[512,2048]{1,0:T(8,128)(2,1)}), bf16[128,2048]{1,0:T(8,128)(2,1)}) %reduce-scatter.5.cloned.1.call-update) | async-done | bytes 524304 | tf_op jit(solution)/shard_map/while/body/eval_jaxpr/reduce_scatter | solution.py:87
  1842.8 44.8 %all-gather.5.cloned.1.call-done = bf16[512,2048]{1,0:T(8,128)(2,1)} async-done(((bf16[128,2048]{1,0:T(8,128)(2,1)}), bf16[512,2048]{1,0:T(8,128)(2,1)}) %all-gather.5.cloned.1.call-update) | async-done | bytes 2097168 | tf_op jit(solution)/shard_map/while/body/eval_jaxpr/all_gather | solution.py:82
  1915.8 42.6 %reduce-scatter.5.cloned.1.call-done = bf16[128,2048]{1,0:T(8,128)(2,1)} async-done(((bf16[512,2048]{1,0:T(8,128)(2,1)}), bf16[128,2048]{1,0:T(8,128)(2,1)}) %reduce-scatter.5.cloned.1.call-update) | async-done | bytes 524304 | tf_op jit(solution)/shard_map/while/body/eval_jaxpr/reduce_scatter | solution.py:87
  2088.1 44.8 %all-gather.5.cloned.1.call-done = bf16[512,2048]{1,0:T(8,128)(2,1)} async-done(((bf16[128,2048]{1,0:T(8,128)(2,1)}), bf16[512,2048]{1,0:T(8,128)(2,1)}) %all-gather.5.cloned.1.call-update) | async-done | bytes 2097168 | tf_op jit(solution)/shard_map/while/body/eval_jaxpr/all_gather | solution.py:82
  2161.0 42.6 %reduce-scatter.5.cloned.1.call-done = bf16[128,2048]{1,0:T(8,128)(2,1)} async-done(((bf16[512,2048]{1,0:T(8,128)(2,1)}), bf16[128,2048]{1,0:T(8,128)(2,1)}) %reduce-scatter.5.cloned.1.call-update) | async-done | bytes 524304 | tf_op jit(solution)/shard_map/while/body/eval_jaxpr/reduce_scatter | solution.py:87
  2333.4 44.8 %all-gather.5.cloned.1.call-done = bf16[512,2048]{1,0:T(8,128)(2,1)} async-done(((bf16[128,2048]{1,0:T(8,128)(2,1)}), bf16[512,2048]{1,0:T(8,128)(2,1)}) %all-gather.5.cloned.1.call-update) | async-done | bytes 2097168 | tf_op jit(solution)/shard_map/while/body/eval_jaxpr/all_gather | solution.py:82
  2406.4 42.6 %reduce-scatter.5.cloned.1.call-done = bf16[128,2048]{1,0:T(8,128)(2,1)} async-done(((bf16[512,2048]{1,0:T(8,128)(2,1)}), bf16[128,2048]{1,0:T(8,128)(2,1)}) %reduce-scatter.5.cloned.1.call-update) | async-done | bytes 524304 | tf_op jit(solution)/shard_map/while/body/eval_jaxpr/reduce_scatter | solution.py:87
  2578.7 44.8 %all-gather.5.cloned.1.call-done = bf16[512,2048]{1,0:T(8,128)(2,1)} async-done(((bf16[128,2048]{1,0:T(8,128)(2,1)}), bf16[512,2048]{1,0:T(8,128)(2,1)}) %all-gather.5.cloned.1.call-update) | async-done | bytes 2097168 | tf_op jit(solution)/shard_map/while/body/eval_jaxpr/all_gather | solution.py:82
  2651.7 42.6 %reduce-scatter.5.cloned.1.call-done = bf16[128,2048]{1,0:T(8,128)(2,1)} async-done(((bf16[512,2048]{1,0:T(8,128)(2,1)}), bf16[128,2048]{1,0:T(8,128)(2,1)}) %reduce-scatter.5.cloned.1.call-update) | async-done | bytes 524304 | tf_op jit(solution)/shard_map/while/body/eval_jaxpr/reduce_scatter | solution.py:87
  2711.2 86.5 %all-reduce.2.cloned.1.call-done = bf16[8,128,2048]{2,1,0:T(8,128)(2,1)} async-done(((bf16[8,128,2048]{2,1,0:T(8,128)(2,1)}), bf16[8,128,2048]{2,1,0:T(8,128)(2,1)}) %all-reduce.2.cloned.1.call-update) | async-done | bytes 4194320 | tf_op jit(solution)/shard_map/psum | solution.py:116
  (570 shorter events, 1737.6 us)
Async XLA Ops:
  12.5 109.7 %reduce-scatter.3.cloned.1.call-start = ((), (), s32[]{:S(2)}) async-start(), calls=%async_computation.4 | async-start | bytes 2621440 | tf_op jit(solution)/shard_map/while/body/eval_jaxpr/reduce_scatter | solution.py:80
  125.6 115.6 %reduce-scatter.5.cloned.1.call-start = ((), (), s32[]{:S(2)}) async-start(), calls=%async_computation.6 | async-start | bytes 2621440 | tf_op jit(solution)/shard_map/while/body/eval_jaxpr/reduce_scatter | solution.py:87
  257.2 110.4 %reduce-scatter.3.cloned.1.call-start = ((), (), s32[]{:S(2)}) async-start(), calls=%async_computation.4 | async-start | bytes 2621440 | tf_op jit(solution)/shard_map/while/body/eval_jaxpr/reduce_scatter | solution.py:80
  370.9 115.6 %reduce-scatter.5.cloned.1.call-start = ((), (), s32[]{:S(2)}) async-start(), calls=%async_computation.6 | async-start | bytes 2621440 | tf_op jit(solution)/shard_map/while/body/eval_jaxpr/reduce_scatter | solution.py:87
  502.5 110.4 %reduce-scatter.3.cloned.1.call-start = ((), (), s32[]{:S(2)}) async-start(), calls=%async_computation.4 | async-start | bytes 2621440 | tf_op jit(solution)/shard_map/while/body/eval_jaxpr/reduce_scatter | solution.py:80
  616.2 115.6 %reduce-scatter.5.cloned.1.call-start = ((), (), s32[]{:S(2)}) async-start(), calls=%async_computation.6 | async-start | bytes 2621440 | tf_op jit(solution)/shard_map/while/body/eval_jaxpr/reduce_scatter | solution.py:87
  747.8 110.4 %reduce-scatter.3.cloned.1.call-start = ((), (), s32[]{:S(2)}) async-start(), calls=%async_computation.4 | async-start | bytes 2621440 | tf_op jit(solution)/shard_map/while/body/eval_jaxpr/reduce_scatter | solution.py:80
  861.5 115.6 %reduce-scatter.5.cloned.1.call-start = ((), (), s32[]{:S(2)}) async-start(), calls=%async_computation.6 | async-start | bytes 2621440 | tf_op jit(solution)/shard_map/while/body/eval_jaxpr/reduce_scatter | solution.py:87
  993.1 110.4 %reduce-scatter.3.cloned.1.call-start = ((), (), s32[]{:S(2)}) async-start(), calls=%async_computation.4 | async-start | bytes 2621440 | tf_op jit(solution)/shard_map/while/body/eval_jaxpr/reduce_scatter | solution.py:80
  1106.8 115.6 %reduce-scatter.5.cloned.1.call-start = ((), (), s32[]{:S(2)}) async-start(), calls=%async_computation.6 | async-start | bytes 2621440 | tf_op jit(solution)/shard_map/while/body/eval_jaxpr/reduce_scatter | solution.py:87
  1238.4 110.4 %reduce-scatter.3.cloned.1.call-start = ((), (), s32[]{:S(2)}) async-start(), calls=%async_computation.4 | async-start | bytes 2621440 | tf_op jit(solution)/shard_map/while/body/eval_jaxpr/reduce_scatter | solution.py:80
  1306.1 90.9 %all-gather.5.cloned.1.call-start = ((), (), s32[]{:S(2)}) async-start(), calls=%async_computation.5 | async-start | bytes 2621440 | tf_op jit(solution)/shard_map/while/body/eval_jaxpr/all_gather | solution.py:82
  1352.1 115.6 %reduce-scatter.5.cloned.1.call-start = ((), (), s32[]{:S(2)}) async-start(), calls=%async_computation.6 | async-start | bytes 2621440 | tf_op jit(solution)/shard_map/while/body/eval_jaxpr/reduce_scatter | solution.py:87
  1483.7 110.3 %reduce-scatter.3.cloned.1.call-start = ((), (), s32[]{:S(2)}) async-start(), calls=%async_computation.4 | async-start | bytes 2621440 | tf_op jit(solution)/shard_map/while/body/eval_jaxpr/reduce_scatter | solution.py:80
  1597.4 115.6 %reduce-scatter.5.cloned.1.call-start = ((), (), s32[]{:S(2)}) async-start(), calls=%async_computation.6 | async-start | bytes 2621440 | tf_op jit(solution)/shard_map/while/body/eval_jaxpr/reduce_scatter | solution.py:87
  1729.0 110.4 %reduce-scatter.3.cloned.1.call-start = ((), (), s32[]{:S(2)}) async-start(), calls=%async_computation.4 | async-start | bytes 2621440 | tf_op jit(solution)/shard_map/while/body/eval_jaxpr/reduce_scatter | solution.py:80
  1842.7 115.6 %reduce-scatter.5.cloned.1.call-start = ((), (), s32[]{:S(2)}) async-start(), calls=%async_computation.6 | async-start | bytes 2621440 | tf_op jit(solution)/shard_map/while/body/eval_jaxpr/reduce_scatter | solution.py:87
  1974.3 110.4 %reduce-scatter.3.cloned.1.call-start = ((), (), s32[]{:S(2)}) async-start(), calls=%async_computation.4 | async-start | bytes 2621440 | tf_op jit(solution)/shard_map/while/body/eval_jaxpr/reduce_scatter | solution.py:80
  2088.0 115.6 %reduce-scatter.5.cloned.1.call-start = ((), (), s32[]{:S(2)}) async-start(), calls=%async_computation.6 | async-start | bytes 2621440 | tf_op jit(solution)/shard_map/while/body/eval_jaxpr/reduce_scatter | solution.py:87
  2219.6 110.4 %reduce-scatter.3.cloned.1.call-start = ((), (), s32[]{:S(2)}) async-start(), calls=%async_computation.4 | async-start | bytes 2621440 | tf_op jit(solution)/shard_map/while/body/eval_jaxpr/reduce_scatter | solution.py:80
  2333.3 115.6 %reduce-scatter.5.cloned.1.call-start = ((), (), s32[]{:S(2)}) async-start(), calls=%async_computation.6 | async-start | bytes 2621440 | tf_op jit(solution)/shard_map/while/body/eval_jaxpr/reduce_scatter | solution.py:87
  2464.9 110.4 %reduce-scatter.3.cloned.1.call-start = ((), (), s32[]{:S(2)}) async-start(), calls=%async_computation.4 | async-start | bytes 2621440 | tf_op jit(solution)/shard_map/while/body/eval_jaxpr/reduce_scatter | solution.py:80
  2578.7 115.6 %reduce-scatter.5.cloned.1.call-start = ((), (), s32[]{:S(2)}) async-start(), calls=%async_computation.6 | async-start | bytes 2621440 | tf_op jit(solution)/shard_map/while/body/eval_jaxpr/reduce_scatter | solution.py:87
  2706.7 91.0 %all-reduce.2.cloned.1.call-start = ((), (), s32[]{:S(2)}) async-start(), calls=%async_computation.2 | async-start | bytes 8388608 | tf_op jit(solution)/shard_map/psum | solution.py:116
  (87 other events, 2403.3 us)
Sparse Core Ops, SparseCore 0:
  12.7 44.2 all-gather.2
  125.7 44.7 all-gather.4
  257.3 44.9 all-gather.2
  371.0 44.7 all-gather.4
  502.6 44.9 all-gather.2
  616.3 44.7 all-gather.4
  747.9 44.9 all-gather.2
  861.6 44.7 all-gather.4
  993.2 44.9 all-gather.2
  1106.9 44.7 all-gather.4
  1238.5 44.9 all-gather.2
  1306.3 42.4 reduce-scatter.2
  1352.2 44.7 all-gather.4
  1483.8 44.9 all-gather.2
  1597.6 44.7 all-gather.4
  1729.1 44.9 all-gather.2
  1842.8 44.7 all-gather.4
  1974.4 44.9 all-gather.2
  2042.2 42.4 reduce-scatter.2
  2088.1 44.7 all-gather.4
  2219.7 44.9 all-gather.2
  2333.5 44.7 all-gather.4
  2465.0 44.9 all-gather.2
  2578.8 44.7 all-gather.4
  (20 shorter events, 847.2 us)
Sparse Core Ops, SparseCore 1:
  2711.2 86.4 all-reduce.1
where the time goes:
time: 2820 us; the launch traced here: 2810 us
  waiting for transfers between devices  2040 us (72%)
  matrix products  461 us (16%)
  other arithmetic  164 us (6%)
  local copies, waits for them, and re-layouts  72.3 us (3%)
  starting transfers between devices  47.2 us (2%)
    all_gather x11, waiting for transfers between devices, stage_layer(): lax.all_gather(rms_norm(mid_state, gain_mlp), 'tp', axis=0, tiled=True)  493 us
    reduce_scatter x11, waiting for transfers between devices, stage_layer(): lax.psum_scatter(down_part, 'tp', scatter_dimension=0, tiled=True)  468 us
    reduce_scatter x11, waiting for transfers between devices, stage_layer(): lax.psum_scatter(attn_part, 'tp', scatter_dimension=0, tiled=True)  468 us
    all_gather x11, waiting for transfers between devices, stage_layer(): lax.all_gather(rms_norm(hidden, gain_attn), 'tp', axis=0, tiled=True)  457 us
    dot_general x11, matrix products, stage_layer(): jnp.dot(hidden_act, w_down, preferred_element_type=jnp.float32)  192 us
    dot_general x11, matrix products, stage_layer(): gate_proj = jnp.dot(full_mlp, w_gate, preferred_element_type=jnp.float32)  117 us
    psum x1, waiting for transfers between devices, stage_program(): return lax.psum(jnp.where(is_last, results, jnp.zeros_like(results)), 'pp')  86.5 us
    ppermute x11, waiting for transfers between devices, stage_tick(): return (lax.ppermute(layer_out, 'pp', perm=fwd_perm), layer_out)  66.9 us
  transfers between devices with their start and end apart: 56, of which 56 were waited for; matrix products, arithmetic and copies ran while one was open for 1% of the time, Pallas kernels for 0%

commit v1 on v0

v1 whole, which is shorter than its diff:
```python
import functools
import math

import jax
import jax.numpy as jnp
import numpy as np
from jax import lax
from jax.experimental import pallas as pl
from jax.experimental.pallas import tpu as pltpu
from jax.sharding import PartitionSpec as P

HEAD_DIM = 128
NORM_EPS = 1e-5
ROPE_THETA = 500000.0
ROPE_FACTOR = 8.0
LOW_FREQ = 1.0
HIGH_FREQ = 4.0
ORIG_CTX = 8192.0
NEG = -1e30
MESH = pl.DeviceIdType.MESH
F32 = jnp.float32
BF16 = jnp.bfloat16


def rope_freqs():
    base_freq = 1.0 / (ROPE_THETA ** (np.arange(0, HEAD_DIM, 2) / HEAD_DIM))
    wavelen = 2.0 * np.pi / base_freq
    smooth = (ORIG_CTX / wavelen - LOW_FREQ) / (HIGH_FREQ - LOW_FREQ)
    blended = (1.0 - smooth) * base_freq / ROPE_FACTOR + smooth * base_freq
    scaled = np.where(wavelen > ORIG_CTX / LOW_FREQ, base_freq / ROPE_FACTOR, blended)
    return np.where(wavelen < ORIG_CTX / HIGH_FREQ, base_freq, scaled)


def kernel(n_stages, x_ref, seg_ref, cols_ref, invf_ref, ga_ref, gm_ref,
           wq_ref, wk_ref, wv_ref, wo_ref, wg_ref, wu_ref, wd_ref,
           out_ref,
           wqkv_hbm, wo_hbm, hin_hbm,
           wg_s, wu_s, wd_s, wst, wost, gb, px, ps, kc, vc, hv, h1b, pacc, oacc, sendb, h2b, act, acc, abuf, qb, ob,
           table, cols, mask,
           wr, wx, wsnd, wfwd, wxs, hin_sem, xs, ag, s1s, s2s, pxr, pxs, psr, s4s, s5s, outr, outf, ofs,
           wst_sem, wost_sem, mlp_sem, hv_sem, cols_sem, gate):
    n_mb, T, D = x_ref.shape
    QL = wq_ref.shape[2]
    FL = wg_ref.shape[2]
    NB = wg_s.shape[0]
    FB = FL // NB
    S = seg_ref.shape[1]
    NJ = S // T
    NH = QL // HEAD_DIM
    N = (n_mb // 2) * NJ
    DB = D // NB
    scale = HEAD_DIM ** -0.5
    RB = 16

    hx = lax.axis_index("dp")
    z = lax.axis_index("tp")
    s = lax.axis_index("pp")
    is_home = (z == 1) | (z == 2)
    is_outer = (z == 0) | (z == 3)
    hb = lax.rem(z + 1, 2) * 0 + (z - 1)
    peer = 3 - z
    outer = 3 * (z - 1)
    inner = 1 + z // 2
    odd = lax.rem(s, 2)

    def rcopy(src, dst, ssem, rsem, **dev):
        return pltpu.make_async_remote_copy(src_ref=src, dst_ref=dst, send_sem=ssem, recv_sem=rsem,
                                            device_id=dev, device_id_type=MESH)

    def local(src, dst, sem):
        return pltpu.make_async_copy(src, dst, sem)

    wqkv_own = (wq_ref, wk_ref, wv_ref, wo_ref)

    def mlp_copies():
        cps = []
        for n in range(NB):
            cps.append(local(wg_ref.at[0, :, pl.ds(n * FB, FB)], wg_s.at[n], mlp_sem.at[0, n]))
            cps.append(local(wu_ref.at[0, :, pl.ds(n * FB, FB)], wu_s.at[n], mlp_sem.at[1, n]))
            cps.append(local(wd_ref.at[0, :, pl.ds(n * DB, DB)], wd_s.at[n], mlp_sem.at[2, n]))
        return cps

    for c in mlp_copies():
        c.start()

    def x_copy(w, home):
        return rcopy(x_ref.at[2 * w + (home - 1)], hin_hbm.at[w * NJ + z], xs.at[w, home - 1],
                     hin_sem.at[w * NJ + z], tp=home)

    def x_start(w):
        for home in (1, 2):
            @pl.when((s == 0) & (z != home))
            def _():
                x_copy(w, home).start()

    def x_wait(w):
        for home in (1, 2):
            @pl.when((s == 0) & (z != home))
            def _():
                x_copy(w, home).wait_send()

    x_start(0)

    def half(ref, m, h):
        rows = (D if m < 3 else QL) // 2
        return ref.at[pl.ds(h * rows, rows), :]

    def wslot(r, m):
        return wqkv_hbm.at[r, m] if m < 3 else wo_hbm.at[r]

    def own_w(m):
        return wqkv_own[m].at[0]

    def o_send(m):
        return rcopy(own_w(m), wslot(0, m), wsnd.at[m], wr.at[0, m], tp=inner)

    def p_send(m):
        return rcopy(half(own_w(m), m, hx), half(wslot(1, m), m, hx), wsnd.at[m], wr.at[1, m], tp=peer)

    def f_send(m):
        return rcopy(half(wslot(0, m), m, hx), half(wslot(2, m), m, hx), wfwd.at[m], wr.at[2, m], tp=peer)

    def x_send(r, m):
        return rcopy(half(wslot(r, m), m, hx), half(wslot(r, m), m, hx), wxs.at[r - 1, m], wx.at[r - 1, m], dp=1 - hx)

    @pl.when(odd == 1)
    def _():
        pl.semaphore_wait(gate, 1)

    @pl.when(is_outer)
    def _():
        for m in range(4):
            o_send(m).start()
        for m in range(4):
            o_send(m).wait_send()

    @pl.when(is_home)
    def _():
        for m in range(4):
            p_send(m).start()
        cps = [local(cols_ref.at[2 * w + hb], cols.at[w], cols_sem.at[w]) for w in range(n_mb // 2)]
        for c in cps:
            c.start()
        for c in cps:
            c.wait()
        lane = lax.broadcasted_iota(jnp.int32, (RB, HEAD_DIM), 1)

        def zero_rows(b, carry):
            for i in range(4):
                kc[i, pl.ds(b * RB, RB), :] = jnp.zeros((RB, QL), BF16)
                vc[i, pl.ds(b * RB, RB), :] = jnp.zeros((RB, QL), BF16)
            return carry
        lax.fori_loop(0, S // RB, zero_rows, 0)

        for w in range(n_mb // 2):
            def table_rows(b, carry, w=w):
                pos = cols[w, pl.ds(b * RB, RB), 0:1].astype(F32)
                ang = pos * invf_ref[0:1, :]
                table[w, pl.ds(b * RB, RB), :] = jnp.where(lane < HEAD_DIM // 2, jnp.cos(ang), jnp.sin(ang))
                return carry
            lax.fori_loop(0, S // RB, table_rows, 0)

        steps = [("p", 0), ("o", 0), ("p", 1), ("p", 2), ("o", 1), ("p", 3), ("f", 0), ("o", 2), ("f", 1), ("f", 2), ("o", 3), ("f", 3)]
        for kind, m in steps:
            if kind == "o":
                o_send(m).wait_recv()
                f_send(m).start()
            elif kind == "p":
                p_send(m).wait_recv()
                x_send(1, m).start()
            else:
                f_send(m).wait_recv()
                x_send(2, m).start()
        for m in range(4):
            x_send(1, m).wait_recv()
            x_send(2, m).wait_recv()
        for m in range(4):
            p_send(m).wait_send()
            f_send(m).wait_send()
            x_send(1, m).wait_send()
            x_send(2, m).wait_send()

    @pl.when(odd == 0)
    def _():
        pl.semaphore_signal(gate, inc=1, device_id={"pp": s + 1}, device_id_type=MESH)

    def pf_qkv(i, m, start):
        sl = lax.rem(3 * i + m, 4)

        @pl.when(i == 0)
        def _():
            c = local(own_w(m), wst.at[sl], wst_sem.at[sl])
            c.start() if start else c.wait()

        @pl.when(i != 0)
        def _():
            c = local(wqkv_hbm.at[lax.rem(i + 3, 4), m], wst.at[sl], wst_sem.at[sl])
            c.start() if start else c.wait()

    def pf_wo(i, start):
        sl = lax.rem(i, 2)

        @pl.when(i == 0)
        def _():
            c = local(own_w(3), wost.at[sl], wost_sem.at[sl])
            c.start() if start else c.wait()

        @pl.when(i != 0)
        def _():
            c = local(wo_hbm.at[lax.rem(i + 3, 4)], wost.at[sl], wost_sem.at[sl])
            c.start() if start else c.wait()

    @pl.when(is_home)
    def _():
        for m in range(3):
            pf_qkv(0, m, True)
        pf_wo(0, True)

    for c in mlp_copies():
        c.wait()

    def hin_copy(u):
        return rcopy(h2b, hin_hbm.at[u], s5s, hin_sem.at[u], pp=lax.rem(s + 1, n_stages))

    def s1_outer(u):
        blk = gb.at[lax.rem(u, 3), pl.ds(pl.multiple_of(hb * T, T), T), :]
        return rcopy(blk, blk, s1s.at[0], ag.at[hb, lax.rem(u, 3)], tp=outer)

    def s1_peer(u):
        blk = gb.at[lax.rem(u, 3), pl.ds(pl.multiple_of(hb * T, T), T), :]
        return rcopy(blk, blk, s1s.at[1], ag.at[hb, lax.rem(u, 3)], tp=peer)

    def s2_copy(u):
        blk = gb.at[lax.rem(u, 3), pl.ds(pl.multiple_of((1 - hb) * T, T), T), :]
        return rcopy(blk, blk, s2s, ag.at[1 - hb, lax.rem(u, 3)], tp=outer)

    def ag_wait(b, u):
        blk = gb.at[lax.rem(u, 3), pl.ds(pl.multiple_of(b * T, T), T), :]
        local(blk, blk, ag.at[b, lax.rem(u, 3)]).wait()

    def s3_copy(u):
        sl = lax.rem(u, 2)
        return rcopy(px.at[sl], px.at[sl], pxs.at[sl], pxr.at[sl], tp=inner)

    def s4_copy(u):
        return rcopy(sendb, ps.at[lax.rem(u, 2)], s4s, psr.at[lax.rem(u, 2)], tp=peer)

    def out_copy(u, mb, j):
        return rcopy(h2b, out_ref.at[mb], s5s, outr.at[mb], tp=j)

    def norm_rows(src, gain, dst):
        hf = src.astype(F32)
        inv = lax.rsqrt(jnp.mean(hf * hf, axis=-1, keepdims=True) + NORM_EPS)
        return (hf * inv * gain.astype(F32)).astype(BF16)

    def attention(u):
        w = u // NJ
        j = lax.rem(u, NJ)
        mb = 2 * w + hb
        row0 = pl.multiple_of(j * T, T)
        from_x = (s == 0) & (j == z)

        @pl.when(from_x)
        def _():
            c = local(x_ref.at[mb], hv, hv_sem)
            c.start()
            c.wait()

        @pl.when(jnp.logical_not(from_x))
        def _():
            hin_copy(u).wait_recv()
            c = local(hin_hbm.at[u], hv, hv_sem)
            c.start()
            c.wait()

        def norm_a(b, carry):
            rows = pl.ds(b * RB, RB)
            abuf[rows, :] = norm_rows(hv[rows, :], ga_ref[0:1, :], None)
            return carry
        lax.fori_loop(0, T // RB, norm_a, 0)

        def mask_rows(b, carry):
            r = pl.ds(b * RB, RB)
            segc = cols[w, pl.ds(row0 + b * RB, RB), 1:2]
            segr = seg_ref[pl.ds(mb, 1), :]
            ti = lax.broadcasted_iota(jnp.int32, (RB, S), 0) + (row0 + b * RB)
            ui = lax.broadcasted_iota(jnp.int32, (RB, S), 1)
            mask[r, :] = jnp.where((segc == segr) & (ui <= ti), 1.0, 0.0)
            return carry
        lax.fori_loop(0, T // RB, mask_rows, 0)

        def rope(val, dst_rows):
            pk = table[w, pl.ds(row0, T), :]
            lane = lax.broadcasted_iota(jnp.int32, (T, HEAD_DIM), 1)
            swapped = pltpu.roll(pk, HEAD_DIM // 2, 1)
            cosw = jnp.where(lane < HEAD_DIM // 2, pk, swapped)
            sinw = jnp.where(lane < HEAD_DIM // 2, -swapped, pk)
            outs = []
            for h in range(NH):
                v = val[:, h * HEAD_DIM:(h + 1) * HEAD_DIM]
                outs.append((v * cosw + pltpu.roll(v, HEAD_DIM // 2, 1) * sinw).astype(BF16))
            return outs

        def shard(i, carry):
            @pl.when((i < 3))
            def _():
                pf_wo(i + 1, True)

            def piece(m):
                pf_qkv(i, m, False)
                val = jnp.dot(abuf[...], wst[lax.rem(3 * i + m, 4)], preferred_element_type=F32)

                @pl.when(i < 3)
                def _():
                    pf_qkv(i + 1, m, True)

                @pl.when((i == 3) & (u < N - 1))
                def _():
                    pf_qkv(0, m, True)
                return val

            for h, val in enumerate(rope(piece(0), None)):
                qb[:, h * HEAD_DIM:(h + 1) * HEAD_DIM] = val
            for h, val in enumerate(rope(piece(1), None)):
                kc[i, pl.ds(row0, T), h * HEAD_DIM:(h + 1) * HEAD_DIM] = val
            vc[i, pl.ds(row0, T), :] = piece(2).astype(BF16)
            for h in range(NH):
                cs = slice(h * HEAD_DIM, (h + 1) * HEAD_DIM)
                sc = lax.dot_general(qb[:, cs], kc[i, :, cs], (((1,), (1,)), ((), ())), preferred_element_type=F32) * scale
                sc = jnp.where(mask[...] > 0.5, sc, NEG)
                e = jnp.exp(sc - jnp.max(sc, axis=-1, keepdims=True))
                p = (e * (1.0 / jnp.sum(e, axis=-1, keepdims=True))).astype(BF16)
                ob[:, cs] = jnp.dot(p, vc[i, :, cs], preferred_element_type=F32).astype(BF16)
            pf_wo(i, False)
            y = jnp.dot(ob[...], wost[lax.rem(i, 2)], preferred_element_type=F32)

            @pl.when(i == 0)
            def _():
                acc[...] = y

            @pl.when(i != 0)
            def _():
                acc[...] = acc[...] + y
            return carry
        lax.fori_loop(0, 4, shard, 0)

        @pl.when(u < N - 1)
        def _():
            pf_wo(0, True)

        def norm_b(b, carry):
            rows = pl.ds(b * RB, RB)
            h1 = (hv[rows, :].astype(F32) + acc[rows, :].astype(BF16).astype(F32)).astype(BF16)
            h1b[lax.rem(u, 3), rows, :] = h1
            gb[lax.rem(u, 3), pl.ds(pl.multiple_of(hb * T + b * RB, RB), RB), :] = norm_rows(h1, gm_ref[0:1, :], None)
            return carry
        lax.fori_loop(0, T // RB, norm_b, 0)

    def mlp(sl):
        def up(n, carry):
            xin = gb[sl]
            g = jnp.dot(xin, wg_s[n], preferred_element_type=F32)
            u_ = jnp.dot(xin, wu_s[n], preferred_element_type=F32)
            act[:, pl.ds(pl.multiple_of(n * FB, FB), FB)] = (jax.nn.silu(g) * u_).astype(BF16)
            return carry
        lax.fori_loop(0, NB, up, 0)

        def down(n, carry):
            pacc[:, pl.ds(pl.multiple_of(n * DB, DB), DB)] = jnp.dot(act[...], wd_s[n], preferred_element_type=F32)
            return carry
        lax.fori_loop(0, NB, down, 0)

    def body(u, carry):
        slot = lax.rem(u, 3)

        @pl.when(is_home)
        def _():
            @pl.when((s == 0) & (lax.rem(u, NJ) == 0) & (u + NJ < N))
            def _():
                for home in (1, 2):
                    @pl.when(z != home)
                    def _():
                        x_copy(u // NJ + 1, home).start()

            @pl.when(u < N)
            def _():
                attention(u)

            @pl.when((u >= 1) & (u <= N))
            def _():
                s1_outer(u - 1).wait_send()
                s1_peer(u - 1).wait_send()

            @pl.when(u < N)
            def _():
                s1_outer(u).start()
                s1_peer(u).start()

            @pl.when((u >= 2) & (u < N + 2))
            def _():
                v = u - 2
                sl = lax.rem(v, 2)
                s3_copy(v).wait_recv()

                @pl.when(v >= 1)
                def _():
                    s4_copy(v - 1).wait_send()

                def comb(b, carry):
                    rows = pl.ds(b * RB, RB)
                    mine = pl.ds(pl.multiple_of(hb * T + b * RB, RB), RB)
                    theirs = pl.ds(pl.multiple_of((1 - hb) * T + b * RB, RB), RB)
                    oacc[rows, :] = pacc[mine, :] + px[sl, mine, :].astype(F32)
                    sendb[rows, :] = (pacc[theirs, :] + px[sl, theirs, :].astype(F32)).astype(BF16)
                    return carry
                lax.fori_loop(0, T // RB, comb, 0)
                s4_copy(v).start()

        @pl.when(is_outer & (u < N))
        def _():
            @pl.when((s == 0) & (lax.rem(u, NJ) == 0) & (u + NJ < N))
            def _():
                for home in (1, 2):
                    x_copy(u // NJ + 1, home).start()
            ag_wait(0, u)
            ag_wait(1, u)

        @pl.when((is_home & (u >= 1) & (u <= N)) | (is_outer & (u < N)))
        def _():
            mlp(lax.rem(u + 2 * (is_home.astype(jnp.int32)), 3))

        @pl.when(is_outer & (u < N))
        def _():
            sl = lax.rem(u, 2)

            @pl.when(u >= 2)
            def _():
                s3_copy(u - 2).wait_send()

            def conv(b, carry):
                rows = pl.ds(b * RB, RB)
                px[sl, rows, :] = pacc[rows, :].astype(BF16)
                return carry
            lax.fori_loop(0, 2 * T // RB, conv, 0)
            s3_copy(u).start()

        @pl.when(is_home)
        def _():
            @pl.when((u >= 1) & (u <= N))
            def _():
                s2_copy(u - 1).wait_send()

            @pl.when(u < N)
            def _():
                ag_wait(1 - hb, u)
                s2_copy(u).start()

            @pl.when((u >= 2) & (u < N + 2))
            def _():
                v = u - 2
                s4_wait = s4_copy(v)
                s4_wait.wait_recv()
                vw = v // NJ
                vj = lax.rem(v, NJ)

                @pl.when(v >= 1)
                def _():
                    hin_copy(v).wait_send()

                def fin(b, carry):
                    rows = pl.ds(b * RB, RB)
                    d = (oacc[rows, :] + ps[lax.rem(v, 2), rows, :].astype(F32)).astype(BF16)
                    h2b[rows, :] = (h1b[lax.rem(v, 3), rows, :].astype(F32) + d.astype(F32)).astype(BF16)
                    return carry
                lax.fori_loop(0, T // RB, fin, 0)

                @pl.when(s < n_stages - 1)
                def _():
                    hin_copy(v).start()

                @pl.when((s == n_stages - 1) & (vj != z))
                def _():
                    out_copy(v, 2 * vw + hb, vj).start()

                @pl.when((s == n_stages - 1) & (vj == z))
                def _():
                    local(h2b, out_ref.at[2 * vw + hb], s5s).start()

        v = u - 4

        @pl.when((s == n_stages - 1) & (v >= 0) & (v < N))
        def _():
            @pl.when(lax.rem(v, NJ) == z)
            def _():
                for b in (0, 1):
                    mb = 2 * (v // NJ) + b

                    @pl.when(z - 1 != b)
                    def _(mb=mb):
                        local(out_ref.at[mb], out_ref.at[mb], outr.at[mb]).wait()
                    for p in range(n_stages - 1):
                        rcopy(out_ref.at[mb], out_ref.at[mb], ofs.at[mb, p], outf, pp=p).start()
        return carry

    lax.fori_loop(0, N + 4, body, 0)

    @pl.when(is_home)
    def _():
        s4_copy(N - 1).wait_send()
        hin_copy(N - 1).wait_send()

    @pl.when(is_outer)
    def _():
        s3_copy(N - 2).wait_send()
        s3_copy(N - 1).wait_send()

    for w in range(n_mb // 2):
        x_wait(w)

    @pl.when(s == n_stages - 1)
    def _():
        for mb in range(n_mb):
            for p in range(n_stages - 1):
                rcopy(out_ref.at[mb], out_ref.at[mb], ofs.at[mb, p], outf, pp=p).wait_send()

    @pl.when(s < n_stages - 1)
    def _():
        rcopy(out_ref, out_ref, ofs.at[0, 0], outf, pp=s).wait_recv()


def solution(mesh):
    n_stages = mesh.shape['pp']

    def stage_program(hidden_in, seg_ids, positions, attn_norm, w_query, w_key, w_value, w_out, mlp_norm, w_gate, w_up, w_down):
        n_mb, T, D = hidden_in.shape
        S = seg_ids.shape[1]
        QL = w_query.shape[2]
        FL = w_gate.shape[2]
        NJ = S // T
        N = (n_mb // 2) * NJ
        NB = max(1, FL // 512)
        cols = jnp.stack([positions, seg_ids], axis=-1)
        invf = jnp.asarray(np.tile(rope_freqs(), 2)[None, :], F32)
        any_spec = pl.BlockSpec(memory_space=pl.ANY)
        vmem = pl.BlockSpec(memory_space=pltpu.VMEM)
        dma = pltpu.SemaphoreType.DMA
        scratch = [
            pltpu.VMEM((NB, D, FL // NB), BF16), pltpu.VMEM((NB, D, FL // NB), BF16), pltpu.VMEM((NB, FL, D // NB), BF16),
            pltpu.VMEM((4, D, QL), BF16), pltpu.VMEM((2, QL, D), BF16),
            pltpu.VMEM((3, 2 * T, D), BF16),
            pltpu.VMEM((2, 2 * T, D), BF16),
            pltpu.VMEM((2, T, D), BF16),
            pltpu.VMEM((4, S, QL), BF16), pltpu.VMEM((4, S, QL), BF16),
            pltpu.VMEM((T, D), BF16),
            pltpu.VMEM((3, T, D), BF16),
            pltpu.VMEM((2 * T, D), F32),
            pltpu.VMEM((T, D), F32),
            pltpu.VMEM((T, D), BF16),
            pltpu.VMEM((T, D), BF16),
            pltpu.VMEM((2 * T, FL), BF16),
            pltpu.VMEM((T, D), F32),
            pltpu.VMEM((T, D), BF16),
            pltpu.VMEM((T, QL), BF16), pltpu.VMEM((T, QL), BF16),
            pltpu.VMEM((n_mb // 2, S, HEAD_DIM), F32),
            pltpu.VMEM((n_mb // 2, S, 2), jnp.int32),
            pltpu.VMEM((T, S), F32),
            dma((3, 4)), dma((2, 4)), dma((4,)), dma((4,)), dma((2, 4)),
            dma((N,)), dma((n_mb // 2, 2)), dma((2, 3)), dma((2,)), dma, dma((2,)), dma((2,)), dma((2,)), dma, dma,
            dma((n_mb,)), dma, dma((n_mb, n_stages - 1)),
            dma((4,)), dma((2,)), dma((3, NB)), dma, dma((n_mb // 2,)),
            pltpu.SemaphoreType.REGULAR,
        ]
        return pl.pallas_call(
            functools.partial(kernel, n_stages),
            out_shape=[jax.ShapeDtypeStruct(hidden_in.shape, BF16), jax.ShapeDtypeStruct((3, 3, D, QL), BF16),
                       jax.ShapeDtypeStruct((3, QL, D), BF16), jax.ShapeDtypeStruct((N, T, D), BF16)],
            in_specs=[any_spec, vmem, any_spec, vmem, vmem, vmem] + [any_spec] * 7,
            out_specs=[any_spec] * 4,
            scratch_shapes=scratch,
            compiler_params=pltpu.CompilerParams(has_side_effects=True, vmem_limit_bytes=67_043_328),
        )(hidden_in, seg_ids, cols, invf, attn_norm, mlp_norm, w_query, w_key, w_value, w_out, w_gate, w_up, w_down)[0]

    act_spec = P('dp', 'tp', None)
    row_spec = P('dp', None)
    gain_spec = P('pp', None)
    col_spec = P('pp', None, 'tp')
    rows_spec = P('pp', 'tp', None)
    return jax.shard_map(stage_program, mesh=mesh,
                         in_specs=(act_spec, row_spec, row_spec, gain_spec, col_spec, col_spec, col_spec, rows_spec, gain_spec, col_spec, col_spec, rows_spec),
                         out_specs=act_spec, check_vma=False)
```

time: 2820 us -> 1180 us (0.42)
  waiting for transfers between devices: 2040 us -> 0 us
  Pallas kernels: 0 us -> 1170 us
  matrix products: 461 us -> 0 us
  other arithmetic: 164 us -> 0.74 us
  local copies, waits for them, and re-layouts: 72.3 us -> 6.75 us
  starting transfers between devices: 47.2 us -> 0 us
    pallas_call x0 -> x1, Pallas kernels: none -> 1170 us  [stage_program(): pl.pallas_call(functools.partial(kernel, n_stages), out_shape=[jax.ShapeD...]
    all_gather x22 -> x0, waiting for transfers between devices: 951 us -> none  [the longest x11 493 us: stage_layer(): lax.all_gather(rms_norm(mid_state, gain_mlp), 'tp', axis=0, tiled=True)]
    reduce_scatter x22 -> x0, waiting for transfers between devices: 936 us -> none  [the longest x11 468 us: stage_layer(): lax.psum_scatter(down_part, 'tp', scatter_dimension=0, tiled=True)]
    dot_general x88 -> x0, matrix products: 461 us -> none  [the longest x11 192 us: stage_layer(): jnp.dot(hidden_act, w_down, preferred_element_type=jnp.float32)]
    psum x1 -> x0, waiting for transfers between devices: 86.5 us -> none  [stage_program(): return lax.psum(jnp.where(is_last, results, jnp.zeros_like(results)), 'pp')]
    ppermute x11 -> x0, waiting for transfers between devices: 66.9 us -> none  [stage_tick(): return (lax.ppermute(layer_out, 'pp', perm=fwd_perm), layer_out)]
    while x154 -> x0, local copies, waits for them, and re-layouts: 50.1 us -> none
    ppermute x11 -> x0, starting transfers between devices: 45.7 us -> none  [stage_tick(): return (lax.ppermute(layer_out, 'pp', perm=fwd_perm), layer_out)]
  transfers between devices with their start and end apart: 56 -> 0, of which waited for: 56 -> 0; matrix products, arithmetic and copies ran while one was open for 1% -> 0% of each run, Pallas kernels for 0% -> 0%
where the time goes in v1:
time: 1180 us
  Pallas kernels  1170 us (99%)
    pallas_call x1, Pallas kernels, stage_program(): pl.pallas_call(functools.partial(kernel, n_stages), out_shape=[jax.ShapeD...  1170 us

profile of v1, /device:TPU:25, one launch (start us, length us, event | category | flops | bytes accessed | tf_op | source)
XLA Modules:
  0.0 1178.2 jit_solution(17995964668551724158)
XLA Ops:
  0.0 0.7 pad_add_fusion
  0.7 2.0 copy.16.cols_ref
  2.7 1170.7 %shard_map.127 = (bf16[8,128,2048]{2,1,0:T(8,128)(2,1)}, bf16[3,3,2048,512]{3,2,1,0:T(8,128)(2,1)}, bf16[3,512,2048]{2,1,0:T(8,128)(2,1)}, bf16[16,128,2048]{2,1,0:T(8,128)(2,1)}) custom-call(bf16[8,128,2048]{2,1,0:T(8,128)(2,1)} %x_ref.1, s32[8,512]{1,0:T(8,128)} %seg_ref.1, s32[8,512,2]{2,1,0:T(8,128)} %copy.16.cols_ref, f32[1,128]{1,0:T(1,128)} %constant.2.clone.invf_ref, ...), custom_call_target="tpu_custom_call" | custom-call | tf_op jit(solution)/shard_map/pallas_call | solution.py:573
  1173.4 4.8 copy.18
